TPU v7x, 32 devices: a whole 2x2x4 slice. The times are simulated.
32 devices in a mesh: section: 8 (over z, core), board: 4 (over y, x).
Axes of the slice: x: 2, y: 2, z: 4, core: 2. Of those that a mesh axis runs over, the one named last changes fastest.
Arguments:
- root_reach: float32 [2, 8, 1326], replicated, may hold values from 0.05 to 1
- frontier_value: float32 [2, 8, 1326], replicated, may hold values from -60 to 60
- regret_stop: float32 [8, 16, 8, 1326], P('section', 'board'), may hold values from 1 to 30
- regret_go: float32 [8, 16, 8, 1326], P('section', 'board'), may hold values from 1 to 30
- board_live: int32 [16], P('board'), may hold values from 0 to 1, as said below
- board_cards: int32 [16, 5], P('board'), may hold values from 0 to 51, as said below
- hand_rank: int32 [16, 1326], P('board'), may hold values from 0 to 1325
Outputs:
- new_stop: float32 [8, 16, 8, 1326], P('section', 'board')
- new_go: float32 [8, 16, 8, 1326], P('section', 'board')
- section_values: float32 [8, 2, 8, 1326], P('section')
Inputs may be any that keep to these rules, and one draw needn't show every extreme that they name: `board_live`: 0 or 1; among each device's 4 slots the first one is always 1. `board_cards`: a slot's 5 cards are distinct. `hand_rank`: equal values tie.
All inputs are finite; a program needn't handle non-finite values.
Results may differ from a plain program's by a relative error of at most 0.0008.
Values sent between devices are 32-bit elements; how exact they have to be, the bound alone decides.
A program may use at most 64 MiB of HBM per device.

v0:
```python
import jax
import jax.numpy as jnp
import numpy as np
from jax import lax
from jax.sharding import PartitionSpec as P

CARDS = 52


def free_pairs():
    first, second = np.triu_indices(CARDS, 1)
    first = jnp.asarray(first.astype(np.int32))
    second = jnp.asarray(second.astype(np.int32))
    shared = (
        (first[:, None] == first[None, :])
        | (first[:, None] == second[None, :])
        | (second[:, None] == first[None, :])
        | (second[:, None] == second[None, :])
    )
    return jnp.where(shared, 0.0, 1.0).astype(jnp.bfloat16)


def board_masks(board_cards):
    first, second = np.triu_indices(CARDS, 1)
    first = jnp.asarray(first.astype(np.int32))
    second = jnp.asarray(second.astype(np.int32))
    hits = (board_cards[:, :, None] == first[None, None, :]) | (
        board_cards[:, :, None] == second[None, None, :]
    )
    return jnp.where(jnp.any(hits, axis=1), 0.0, 1.0).astype(jnp.float32)


def showdown(reach_one, stop_weight, mask_row, rank_row, disjoint):
    leaf_reach = (reach_one * stop_weight).astype(jnp.bfloat16)
    mask_half = mask_row.astype(jnp.bfloat16)
    payoff = (
        jnp.sign(rank_row[:, None] - rank_row[None, :]).astype(jnp.bfloat16)
        * disjoint
        * mask_half[:, None]
        * mask_half[None, :]
    )
    flipped = leaf_reach[::-1].reshape(-1, leaf_reach.shape[-1])
    result = jnp.einsum("rk,hk->rh", flipped, payoff, preferred_element_type=jnp.float32)
    return result.reshape(leaf_reach.shape)


def local(root_reach, frontier_value, regret_stop, regret_go, board_live, board_cards, hand_rank):
    section_idx = lax.axis_index("section")
    players = jnp.arange(2)[:, None, None]
    acting = players == section_idx % 2
    masks = board_masks(board_cards)
    alive = board_live > 0
    alive_weight = alive.astype(jnp.float32)
    stop_now = regret_stop[0]
    go_now = regret_go[0]
    regret_sum = stop_now + go_now
    stop_prob = stop_now / regret_sum
    go_prob = go_now / regret_sum
    factor = jnp.where(acting[None], go_prob[:, None], 1.0)
    stop_weight = jnp.where(acting[None], stop_prob[:, None], 1.0)
    root_masked = root_reach[None] * masks[:, None, None, :]
    factor_all = lax.all_gather(factor[None], "section", axis=0, tiled=True)
    levels = jnp.arange(factor_all.shape[0])[:, None, None, None, None]
    reach_now = root_masked * jnp.prod(jnp.where(levels < section_idx, factor_all, 1.0), axis=0)
    disjoint = free_pairs()
    leaf_list = []
    for slot in range(masks.shape[0]):
        leaf_one = showdown(
            reach_now[slot], stop_weight[slot], masks[slot], hand_rank[slot], disjoint
        )
        leaf_list.append(leaf_one)
    leaf_values = jnp.stack(leaf_list)
    weighted = stop_weight * leaf_values
    frontier_masked = frontier_value[None] * masks[:, None, None, :]
    leaf_all = lax.all_gather(weighted[None], "section", axis=0, tiled=True)
    section_total = leaf_all.shape[0]

    def climb(position, carried):
        level_now = section_total - 1 - position
        updated = leaf_all[level_now] + factor_all[level_now] * carried
        return jnp.where(level_now > section_idx, updated, carried)

    value_next = lax.fori_loop(0, section_total, climb, frontier_masked)
    node_value = weighted + factor * value_next
    section_part = jnp.sum(alive_weight[:, None, None, None] * node_value, axis=0)
    live_part = jnp.sum(alive_weight)
    section_sum, live_total = lax.psum((section_part, live_part), "board")
    section_value = section_sum / live_total
    own_next = jnp.sum(jnp.where(acting[None], value_next, 0.0), axis=1)
    own_leaf = jnp.sum(jnp.where(acting[None], leaf_values, 0.0), axis=1)
    gap = own_leaf - own_next
    keep_slot = alive[:, None, None]
    new_stop = jnp.where(keep_slot, jnp.maximum(stop_now + go_prob * gap, 0.0), stop_now)
    new_go = jnp.where(keep_slot, jnp.maximum(go_now - stop_prob * gap, 0.0), go_now)
    return (new_stop[None], new_go[None], section_value[None])


def solution(mesh):
    return jax.shard_map(
        local,
        mesh=mesh,
        in_specs=(
            P(),
            P(),
            P("section", "board", None, None),
            P("section", "board", None, None),
            P("board"),
            P("board", None),
            P("board", None),
        ),
        out_specs=(
            P("section", "board", None, None),
            P("section", "board", None, None),
            P("section", None, None, None),
        ),
        check_vma=False,
    )
```

profile of v0, /device:TPU:0, one launch (start us, length us, event | category | flops | bytes accessed | tf_op | source)
XLA Modules:
  0.0 163.7 jit_solution(3219703104629716634)
XLA Ops:
  7.3 1.0 add_divide_fusion.1
  8.3 0.8 broadcast_select_fusion.1
  9.2 0.8 copy.14
  10.0 0.8 or_reduce_fusion
  10.8 0.1 fusion.53
  10.9 0.9 slice_reduce_fusion.3
  11.9 0.1 broadcast_select_fusion
  12.0 36.4 %all-gather.3.cloned.1.call-done = f32[8,4,2,8,1326]{4,3,2,1,0:T(8,128)} async-done(((f32[1,4,2,8,1326]{4,3,2,1,0:T(8,128)}), f32[8,4,2,8,1326]{4,3,2,1,0:T(8,128)}) %all-gather.3.cloned.1.call-update) | async-done | bytes 2715664 | tf_op jit(solution)/shard_map/all_gather | solution.py:62
  48.3 2.1 %select_reduce_fusion = f32[4,2,8,1326]{3,2,1,0:T(8,128)S(1)} fusion(f32[8,4,2,8,1326]{4,3,2,1,0:T(8,128)} %all-gather.3.cloned.1.call-done, pred[8]{0:T(512)(128)(4,1)S(1)} %iota_compare_fusion), kind=kLoop, calls=%fused_computation.28 | loop fusion | flops 1272960 | bytes 3055112 | tf_op jit(solution)/shard_map/reduce_prod | solution.py:64
  50.5 0.1 multiply_multiply_fusion
  50.6 0.1 fusion.46
  50.7 3.7 %fusion.24 = f32[2,8,1326]{2,1,0:T(8,128)S(1)} fusion(bf16[2,8,1326]{2,1,0:T(8,128)(2,1)S(1)} %rev.12, s32[1326]{0:T(1024)S(1)} %get-tuple-element.143, s32[1326]{0:T(1024)S(1)} %copy-done.5, s32[1326]{0:T(1024)S(1)} %copy-done.4, bf16[1326]{0:T(1024)(128)(2,1)S(1)} %get-tuple-element.139), kind=kOutput, calls=%fused_computation.27 | convolution fusion | flops 91430352 | bytes 145860 | tf_op jit(solution)/shard_map/rk,hk->rh/dot_general | solution.py:43
  54.4 3.7 %fusion.22 = f32[2,8,1326]{2,1,0:T(8,128)S(1)} fusion(bf16[2,8,1326]{2,1,0:T(8,128)(2,1)S(1)} %rev.13, s32[1326]{0:T(1024)S(1)} %get-tuple-element.144, s32[1326]{0:T(1024)S(1)} %copy-done.5, s32[1326]{0:T(1024)S(1)} %copy-done.4, bf16[1326]{0:T(1024)(128)(2,1)S(1)} %get-tuple-element.142), kind=kOutput, calls=%fused_computation.26 | convolution fusion | flops 91430352 | bytes 145860 | tf_op jit(solution)/shard_map/rk,hk->rh/dot_general | solution.py:43
  58.1 3.7 %fusion.20 = f32[2,8,1326]{2,1,0:T(8,128)S(1)} fusion(bf16[2,8,1326]{2,1,0:T(8,128)(2,1)S(1)} %rev.14, s32[1326]{0:T(1024)S(1)} %get-tuple-element.146, s32[1326]{0:T(1024)S(1)} %copy-done.5, s32[1326]{0:T(1024)S(1)} %copy-done.4, bf16[1326]{0:T(1024)(128)(2,1)S(1)} %get-tuple-element.141), kind=kOutput, calls=%fused_computation.25 | convolution fusion | flops 91430352 | bytes 145860 | tf_op jit(solution)/shard_map/rk,hk->rh/dot_general | solution.py:43
  61.8 3.9 %fusion.18 = f32[2,8,1326]{2,1,0:T(8,128)S(1)} fusion(bf16[2,8,1326]{2,1,0:T(8,128)(2,1)S(1)} %rev.15, s32[1326]{0:T(1024)S(1)} %get-tuple-element.145, s32[1326]{0:T(1024)S(1)} %copy-done.5, s32[1326]{0:T(1024)S(1)} %copy-done.4, bf16[1326]{0:T(1024)(128)(2,1)S(1)} %get-tuple-element.140), kind=kOutput, calls=%fused_computation.24 | convolution fusion | flops 91430352 | bytes 145860 | tf_op jit(solution)/shard_map/rk,hk->rh/dot_general | solution.py:43
  65.7 0.8 maximum_multiply_fusion
  66.6 0.6 convert_reduce_fusion
  67.2 10.5 %psum.15 = f32[]{:T(128)} all-reduce(f32[]{:T(128)} %convert_reduce_fusion), channel_id=1, replica_groups=mesh['section'=8,'board'=4] {'board'}, use_global_device_ids=true, to_apply=%region_9.10 | all-reduce | flops 1 | bytes 8 | tf_op jit(solution)/shard_map/psum | solution.py:87
  77.8 23.9 %all-gather.5.cloned.1.call-done = f32[8,4,2,8,1326]{4,3,2,1,0:T(8,128)} async-done(((f32[1,4,2,8,1326]{4,3,2,1,0:T(8,128)}), f32[8,4,2,8,1326]{4,3,2,1,0:T(8,128)}) %all-gather.5.cloned.1.call-update) | async-done | bytes 2715664 | tf_op jit(solution)/shard_map/all_gather | solution.py:75
  101.7 11.1 %while.15 = (s32[]{:T(128)}, f32[4,2,8,1326]{3,2,1,0:T(8,128)S(1)}, s32[]{:T(128)}, f32[8,4,2,8,1326]{4,3,2,1,0:T(8,128)}, f32[8,4,2,8,1326]{4,3,2,1,0:T(8,128)}...) while((s32[]{:T(128)}, f32[4,2,8,1326]{3,2,1,0:T(8,128)S(1)}, s32[]{:T(128)}, ...), condition=%wide.region_4.5_spmd, body=%wide.region_3.4_spmd.sunk | while | flops 254599 | bytes 1357977 | solution.py:83
  101.7 1.4 fusion.68
  103.1 1.4 fusion.68
  104.5 1.4 fusion.68
  105.9 1.4 fusion.68
  107.3 1.4 fusion.68
  108.7 1.4 fusion.68
  110.1 1.4 fusion.68
  111.5 1.4 fusion.68
  112.8 0.9 multiply_reduce_fusion
  113.7 0.8 fusion.41
  114.6 40.3 %all-reduce.2.cloned.1.call-done = f32[2,8,1326]{2,1,0:T(8,128)} async-done(((f32[2,8,1326]{2,1,0:T(8,128)}), f32[2,8,1326]{2,1,0:T(8,128)}) %all-reduce.2.cloned.1.call-update) | async-done | bytes 84880 | tf_op jit(solution)/shard_map/psum | solution.py:87
  154.9 2.2 %divide_bitcast_fusion = f32[1,2,8,1326]{3,2,1,0:T(8,128)} fusion(f32[2,8,1326]{2,1,0:T(8,128)} %all-reduce.2.cloned.1.call-done, f32[]{:T(128)} %psum.15), kind=kLoop, calls=%fused_computation.67 | loop fusion | flops 21216 | bytes 169732 | tf_op jit(solution)/shard_map/broadcast_in_dim | solution.py:95
  (28 shorter events, 0.3 us)
Async XLA Ops:
  7.2 43.3 %copy-start.2 = (f32[2,8,1326]{2,1,0:T(8,128)S(1)}, f32[2,8,1326]{2,1,0:T(8,128)}, u32[]{:S(2)}) copy-start(f32[2,8,1326]{2,1,0:T(8,128)} %param.13) | copy-start | bytes 254596
  7.2 43.3 %copy-start.3 = (f32[2,8,1326]{2,1,0:T(8,128)S(1)}, f32[2,8,1326]{2,1,0:T(8,128)}, u32[]{:S(2)}) copy-start(f32[2,8,1326]{2,1,0:T(8,128)} %param.14) | copy-start | bytes 254596
  7.2 41.2 %all-gather.3.cloned.1.call-start = ((), (), s32[]{:S(2)}) async-start(), calls=%async_computation | async-start | bytes 3244032 | tf_op jit(solution)/shard_map/all_gather | solution.py:62
  9.2 92.5 %all-gather.5.cloned.1.call-start = ((), (), s32[]{:S(2)}) async-start(), calls=%async_computation.1 | async-start | bytes 3244032 | tf_op jit(solution)/shard_map/all_gather | solution.py:75
  12.0 38.7 %copy-start.4 = (s32[1326]{0:T(1024)S(1)}, s32[1326]{0:T(1024)}, u32[]{:S(2)}) copy-start(s32[1326]{0:T(1024)} %constant.74.clone) | copy-start | bytes 15916
  12.0 38.7 %copy-start.5 = (s32[1326]{0:T(1024)S(1)}, s32[1326]{0:T(1024)}, u32[]{:S(2)}) copy-start(s32[1326]{0:T(1024)} %constant.75.clone) | copy-start | bytes 15916
  61.8 4.8 %copy-start.6 = (s32[4]{0:T(128)S(1)}, s32[4]{0:T(128)}, u32[]{:S(2)}) copy-start(s32[4]{0:T(128)} %param.17) | copy-start | bytes 52
  66.6 88.3 %all-reduce.2.cloned.1.call-start = ((), (), s32[]{:S(2)}) async-start(), calls=%async_computation.2 | async-start | bytes 180224 | tf_op jit(solution)/shard_map/psum | solution.py:87
  101.7 12.0 %copy-start = (f32[1,4,8,1326]{3,2,1,0:T(8,128)S(1)}, f32[1,4,8,1326]{3,2,1,0:T(8,128)}, u32[]{:S(2)}) copy-start(f32[1,4,8,1326]{3,2,1,0:T(8,128)} %param.16) | copy-start | bytes 509188
  101.7 12.0 %copy-start.1 = (f32[1,4,8,1326]{3,2,1,0:T(8,128)S(1)}, f32[1,4,8,1326]{3,2,1,0:T(8,128)}, u32[]{:S(2)}) copy-start(f32[1,4,8,1326]{3,2,1,0:T(8,128)} %param.15) | copy-start | bytes 509188
Sparse Core Ops, SparseCore 0:
  9.6 38.6 all-gather.2
  66.7 34.9 all-gather.4
  113.8 41.0 all-reduce.1
where the time goes:
time: 164 us
  waiting for transfers between devices  101 us (62%)
  other arithmetic  21.4 us (13%)
  matrix products  15 us (9%)
  between operations  13.9 us (8%)
  blocking collectives  10.5 us (6%)
  local copies, waits for them, and re-layouts  1.84 us (1%)
    psum x1, waiting for transfers between devices, local(): section_sum, live_total = lax.psum((section_part, live_part), 'board')  40.3 us
    all_gather x1, waiting for transfers between devices, local(): factor_all = lax.all_gather(factor[None], 'section', axis=0, tiled=True)  36.4 us
    all_gather x1, waiting for transfers between devices, local(): leaf_all = lax.all_gather(weighted[None], 'section', axis=0, tiled=True)  23.9 us
    dot_general x4, matrix products, showdown(): jnp.einsum('rk,hk->rh', flipped, payoff, preferred_element_type=jnp.float32)  15 us
    select_n x8, other arithmetic, climb(): return jnp.where(level_now > section_idx, updated, carried)  10.9 us
    psum x1, blocking collectives, local(): section_sum, live_total = lax.psum((section_part, live_part), 'board')  10.5 us
  transfers between devices with their start and end apart: 3, of which 3 were waited for; matrix products, arithmetic and copies ran while one was open for 3% of the time, Pallas kernels for 0%

commit v1 on v0

--- a/solution.py
+++ b/solution.py
@@ -59,7 +59,10 @@
     factor = jnp.where(acting[None], go_prob[:, None], 1.0)
     stop_weight = jnp.where(acting[None], stop_prob[:, None], 1.0)
     root_masked = root_reach[None] * masks[:, None, None, :]
-    factor_all = lax.all_gather(factor[None], "section", axis=0, tiled=True)
+    factor_all = jnp.concatenate(
+        lax.all_to_all(jnp.stack([factor[None]] * lax.axis_size("section")), "section", 0, 0),
+        axis=0,
+    )
     levels = jnp.arange(factor_all.shape[0])[:, None, None, None, None]
     reach_now = root_masked * jnp.prod(jnp.where(levels < section_idx, factor_all, 1.0), axis=0)
     disjoint = free_pairs()

time: 164 us -> 207 us (1.26)
  waiting for transfers between devices: 101 us -> 127 us
  local copies, waits for them, and re-layouts: 1.84 us -> 8.68 us
  starting transfers between devices: 0.12 us -> 6.58 us
    all_to_all x0 -> x1, waiting for transfers between devices: none -> 64.3 us  [local(): lax.all_to_all(jnp.stack([factor[None]] * lax.axis_size('section')), 'sec...]
    all_gather x1 -> x0, waiting for transfers between devices: 36.4 us -> none  [local(): factor_all = lax.all_gather(factor[None], 'section', axis=0, tiled=True)]
    all_to_all x0 -> x1, starting transfers between devices: none -> 6.5 us  [local(): lax.all_to_all(jnp.stack([factor[None]] * lax.axis_size('section')), 'sec...]
    rev x4, local copies, waits for them, and re-layouts: 0.02 us -> 4.05 us  [showdown(): flipped = leaf_reach[::-1].reshape(-1, leaf_reach.shape[-1])]
  transfers between devices with their start and end apart: 3 -> 3, of which waited for: 3 -> 3; matrix products, arithmetic and copies ran while one was open for 3% -> 2% of each run, Pallas kernels for 0% -> 0%
where the time goes in v1:
time: 207 us; the launch traced here: 206 us
  waiting for transfers between devices  127 us (61%)
  other arithmetic  22.5 us (11%)
  matrix products  15.8 us (8%)
  between operations  14.3 us (7%)
  blocking collectives  10.5 us (5%)
  local copies, waits for them, and re-layouts  8.68 us (4%)
  starting transfers between devices  6.58 us (3%)
    all_to_all x1, waiting for transfers between devices, local(): lax.all_to_all(jnp.stack([factor[None]] * lax.axis_size('section')), 'sec...  64.3 us
    psum x1, waiting for transfers between devices, local(): section_sum, live_total = lax.psum((section_part, live_part), 'board')  39.3 us
    all_gather x1, waiting for transfers between devices, local(): leaf_all = lax.all_gather(weighted[None], 'section', axis=0, tiled=True)  23.8 us
    dot_general x4, matrix products, showdown(): jnp.einsum('rk,hk->rh', flipped, payoff, preferred_element_type=jnp.float32)  15.8 us
    psum x1, blocking collectives, local(): section_sum, live_total = lax.psum((section_part, live_part), 'board')  10.5 us
    select_n x8, other arithmetic, climb(): return jnp.where(level_now > section_idx, updated, carried)  10 us
    all_to_all x1, starting transfers between devices, local(): lax.all_to_all(jnp.stack([factor[None]] * lax.axis_size('section')), 'sec...  6.5 us
  transfers between devices with their start and end apart: 3, of which 3 were waited for; matrix products, arithmetic and copies ran while one was open for 2% of the time, Pallas kernels for 0%

profile of v1, /device:TPU:0, one launch (start us, length us, event | category | flops | bytes accessed | tf_op | source)
XLA Modules:
  0.0 206.0 jit_solution(17584154837732667624)
XLA Ops:
  7.2 1.0 add_divide_fusion.1
  8.3 0.7 copy-done
  8.9 0.9 broadcast_select_fusion.1
  9.8 1.8 stack.16
  11.6 6.5 %all-to-all-start = ((f32[8,1,4,2,8,1326]{5,4,3,2,1,0:T(8,128)}), f32[8,1,4,2,8,1326]{5,4,3,2,1,0:T(8,128)S(1)}, u32[]{:S(2)}, u32[]{:S(2)}) async-start(f32[8,1,4,2,8,1326]{5,4,3,2,1,0:T(8,128)} %stack.16), calls=%async_computation | async-start | bytes 5767168 | tf_op jit(solution)/shard_map/all_to_all | solution.py:63
  18.5 0.7 fusion.53
  19.1 0.7 slice_reduce_fusion.3
  19.8 64.3 %all-to-all-done = f32[8,1,4,2,8,1326]{5,4,3,2,1,0:T(8,128)S(1)} async-done(((f32[8,1,4,2,8,1326]{5,4,3,2,1,0:T(8,128)}), f32[8,1,4,2,8,1326]{5,4,3,2,1,0:T(8,128)S(1)}, u32[]{:S(2)}, u32[]{:S(2)}) %all-to-all-start) | async-done | bytes 2715680 | tf_op jit(solution)/shard_map/all_to_all | solution.py:63
  84.3 1.0 multiply_multiply_fusion
  85.3 1.7 fusion.46
  87.0 1.4 rev.12
  88.4 1.4 rev.13
  91.0 4.5 %fusion.24 = f32[2,8,1326]{2,1,0:T(8,128)S(1)} fusion(bf16[2,8,1326]{2,1,0:T(8,128)(2,1)} %rev.12, s32[1326]{0:T(1024)} %get-tuple-element.143, s32[1326]{0:T(1024)S(1)} %copy-done.10, s32[1326]{0:T(1024)S(1)} %copy-done.9, bf16[1326]{0:T(1024)(128)(2,1)} %get-tuple-element.139), kind=kOutput, calls=%fused_computation.27 | convolution fusion | flops 91430352 | bytes 145860 | tf_op jit(solution)/shard_map/rk,hk->rh/dot_general | solution.py:43
  95.6 3.7 %fusion.22 = f32[2,8,1326]{2,1,0:T(8,128)S(1)} fusion(bf16[2,8,1326]{2,1,0:T(8,128)(2,1)S(1)} %copy-done.7, s32[1326]{0:T(1024)S(1)} %copy-done.13, s32[1326]{0:T(1024)S(1)} %copy-done.10, s32[1326]{0:T(1024)S(1)} %copy-done.9, bf16[1326]{0:T(1024)(128)(2,1)S(1)} %copy-done.18), kind=kOutput, calls=%fused_computation.26 | convolution fusion | flops 91430352 | bytes 145860 | tf_op jit(solution)/shard_map/rk,hk->rh/dot_general | solution.py:43
  99.4 3.7 %fusion.20 = f32[2,8,1326]{2,1,0:T(8,128)S(1)} fusion(bf16[2,8,1326]{2,1,0:T(8,128)(2,1)S(1)} %copy-done.6, s32[1326]{0:T(1024)S(1)} %copy-done.12, s32[1326]{0:T(1024)S(1)} %copy-done.10, s32[1326]{0:T(1024)S(1)} %copy-done.9, bf16[1326]{0:T(1024)(128)(2,1)S(1)} %copy-done.17), kind=kOutput, calls=%fused_computation.25 | convolution fusion | flops 91430352 | bytes 145860 | tf_op jit(solution)/shard_map/rk,hk->rh/dot_general | solution.py:43
  103.1 3.9 %fusion.18 = f32[2,8,1326]{2,1,0:T(8,128)S(1)} fusion(bf16[2,8,1326]{2,1,0:T(8,128)(2,1)S(1)} %copy-done.5, s32[1326]{0:T(1024)S(1)} %copy-done.11, s32[1326]{0:T(1024)S(1)} %copy-done.10, s32[1326]{0:T(1024)S(1)} %copy-done.9, bf16[1326]{0:T(1024)(128)(2,1)S(1)} %copy-done.16), kind=kOutput, calls=%fused_computation.24 | convolution fusion | flops 91430352 | bytes 145860 | tf_op jit(solution)/shard_map/rk,hk->rh/dot_general | solution.py:43
  107.7 0.9 maximum_multiply_fusion
  109.2 10.5 %psum.15 = f32[]{:T(128)} all-reduce(f32[]{:T(128)} %convert_reduce_fusion), channel_id=1, replica_groups=mesh['section'=8,'board'=4] {'board'}, use_global_device_ids=true, to_apply=%region_9.10 | all-reduce | flops 1 | bytes 8 | tf_op jit(solution)/shard_map/psum | solution.py:90
  119.8 23.8 %all-gather.2.cloned.1.call-done = f32[8,4,2,8,1326]{4,3,2,1,0:T(8,128)} async-done(((f32[1,4,2,8,1326]{4,3,2,1,0:T(8,128)}), f32[8,4,2,8,1326]{4,3,2,1,0:T(8,128)}) %all-gather.2.cloned.1.call-update) | async-done | bytes 2715664 | tf_op jit(solution)/shard_map/all_gather | solution.py:78
  143.6 10.2 %while.15 = (s32[]{:T(128)}, f32[4,2,8,1326]{3,2,1,0:T(8,128)S(1)}, s32[]{:T(128)}, f32[8,4,2,8,1326]{4,3,2,1,0:T(8,128)}, f32[8,4,2,8,1326]{4,3,2,1,0:T(8,128)S...) while((s32[]{:T(128)}, f32[4,2,8,1326]{3,2,1,0:T(8,128)S(1)}, s32[]{:T(128)}, ...), condition=%wide.region_4.5_spmd, body=%wide.region_3.4_spmd.sunk | while | flops 254599 | bytes 1357977 | solution.py:86
  143.6 1.2 fusion.68
  144.9 1.3 fusion.68
  146.1 1.3 fusion.68
  147.4 1.3 fusion.68
  148.7 1.3 fusion.68
  150.0 1.3 fusion.68
  151.3 1.3 fusion.68
  152.5 1.3 fusion.68
  153.8 1.9 multiply_reduce_fusion
  155.8 1.9 fusion.41
  157.6 39.3 %all-reduce.2.cloned.1.call-done = f32[2,8,1326]{2,1,0:T(8,128)} async-done(((f32[2,8,1326]{2,1,0:T(8,128)}), f32[2,8,1326]{2,1,0:T(8,128)}) %all-reduce.2.cloned.1.call-update) | async-done | bytes 84880 | tf_op jit(solution)/shard_map/psum | solution.py:90
  197.0 2.2 %divide_bitcast_fusion = f32[1,2,8,1326]{3,2,1,0:T(8,128)} fusion(f32[2,8,1326]{2,1,0:T(8,128)} %all-reduce.2.cloned.1.call-done, f32[]{:T(128)} %psum.15), kind=kLoop, calls=%fused_computation.67 | loop fusion | flops 21216 | bytes 169732 | tf_op jit(solution)/shard_map/broadcast_in_dim | solution.py:98
  (55 shorter events, 3.2 us)
Async XLA Ops:
  7.2 2.6 %copy-start.14 = (pred[2]{0:T(512)(128)(4,1)}, pred[2]{0:T(512)(128)(4,1)S(1)}, u32[]{:S(2)}) copy-start(pred[2]{0:T(512)(128)(4,1)S(1)} %iota_compare_fusion.1) | copy-start | bytes 10
  8.2 0.7 copy-start
  11.6 6.6 %copy-start.19 = (s32[4,5]{1,0:T(4,128)S(1)}, s32[4,5]{1,0:T(4,128)}, u32[]{:S(2)}) copy-start(s32[4,5]{1,0:T(4,128)} %param.18) | copy-start | bytes 244
  11.6 6.7 %copy-start.9 = (s32[1326]{0:T(1024)S(1)}, s32[1326]{0:T(1024)}, u32[]{:S(2)}) copy-start(s32[1326]{0:T(1024)} %constant.74.clone) | copy-start | bytes 15916
  11.6 6.7 %copy-start.10 = (s32[1326]{0:T(1024)S(1)}, s32[1326]{0:T(1024)}, u32[]{:S(2)}) copy-start(s32[1326]{0:T(1024)} %constant.75.clone) | copy-start | bytes 15916
  11.6 7.5 %copy-start.8 = (s32[4,1326]{1,0:T(4,128)S(1)}, s32[4,1326]{1,0:T(4,128)}, u32[]{:S(2)}) copy-start(s32[4,1326]{1,0:T(4,128)} %param.19) | copy-start | bytes 63652
  11.6 72.4 %all-to-all-start = ((f32[8,1,4,2,8,1326]{5,4,3,2,1,0:T(8,128)}), f32[8,1,4,2,8,1326]{5,4,3,2,1,0:T(8,128)S(1)}, u32[]{:S(2)}, u32[]{:S(2)}) async-start(f32[8,1,4,2,8,1326]{5,4,3,2,1,0:T(8,128)} %stack.16), calls=%async_computation | async-start | bytes 5767168 | tf_op jit(solution)/shard_map/all_to_all | solution.py:63
  18.1 66.2 %copy-start.4 = (f32[2,8,1326]{2,1,0:T(8,128)S(1)}, f32[2,8,1326]{2,1,0:T(8,128)}, u32[]{:S(2)}) copy-start(f32[2,8,1326]{2,1,0:T(8,128)} %param.13) | copy-start | bytes 254596
  18.1 125.4 %all-gather.2.cloned.1.call-start = ((), (), s32[]{:S(2)}) async-start(), calls=%async_computation.1 | async-start | bytes 3244032 | tf_op jit(solution)/shard_map/all_gather | solution.py:78
  91.0 4.5 %copy-start.7 = (bf16[2,8,1326]{2,1,0:T(8,128)(2,1)S(1)}, bf16[2,8,1326]{2,1,0:T(8,128)(2,1)}, u32[]{:S(2)}) copy-start(bf16[2,8,1326]{2,1,0:T(8,128)(2,1)} %rev.13) | copy-start | bytes 127300
  91.0 4.5 %copy-start.13 = (s32[1326]{0:T(1024)S(1)}, s32[1326]{0:T(1024)}, u32[]{:S(2)}) copy-start(s32[1326]{0:T(1024)} %get-tuple-element.144) | copy-start | bytes 15916
  91.0 4.5 %copy-start.18 = (bf16[1326]{0:T(1024)(128)(2,1)S(1)}, bf16[1326]{0:T(1024)(128)(2,1)}, u32[]{:S(2)}) copy-start(bf16[1326]{0:T(1024)(128)(2,1)} %get-tuple-element.142) | copy-start | bytes 7960
  95.6 3.7 %copy-start.6 = (bf16[2,8,1326]{2,1,0:T(8,128)(2,1)S(1)}, bf16[2,8,1326]{2,1,0:T(8,128)(2,1)}, u32[]{:S(2)}) copy-start(bf16[2,8,1326]{2,1,0:T(8,128)(2,1)} %rev.14) | copy-start | bytes 127300
  95.6 3.7 %copy-start.12 = (s32[1326]{0:T(1024)S(1)}, s32[1326]{0:T(1024)}, u32[]{:S(2)}) copy-start(s32[1326]{0:T(1024)} %get-tuple-element.146) | copy-start | bytes 15916
  95.6 3.7 %copy-start.17 = (bf16[1326]{0:T(1024)(128)(2,1)S(1)}, bf16[1326]{0:T(1024)(128)(2,1)}, u32[]{:S(2)}) copy-start(bf16[1326]{0:T(1024)(128)(2,1)} %get-tuple-element.141) | copy-start | bytes 7960
  99.3 7.7 %copy-start.1 = (f32[2,8,1326]{2,1,0:T(8,128)}, f32[2,8,1326]{2,1,0:T(8,128)S(1)}, u32[]{:S(2)}) copy-start(f32[2,8,1326]{2,1,0:T(8,128)S(1)} %fusion.22) | copy-start | bytes 254596
  99.4 3.7 %copy-start.5 = (bf16[2,8,1326]{2,1,0:T(8,128)(2,1)S(1)}, bf16[2,8,1326]{2,1,0:T(8,128)(2,1)}, u32[]{:S(2)}) copy-start(bf16[2,8,1326]{2,1,0:T(8,128)(2,1)} %rev.15) | copy-start | bytes 127300
  99.4 3.7 %copy-start.11 = (s32[1326]{0:T(1024)S(1)}, s32[1326]{0:T(1024)}, u32[]{:S(2)}) copy-start(s32[1326]{0:T(1024)} %get-tuple-element.145) | copy-start | bytes 15916
  99.4 3.7 %copy-start.16 = (bf16[1326]{0:T(1024)(128)(2,1)S(1)}, bf16[1326]{0:T(1024)(128)(2,1)}, u32[]{:S(2)}) copy-start(bf16[1326]{0:T(1024)(128)(2,1)} %get-tuple-element.140) | copy-start | bytes 7960
  103.1 3.9 %copy-start.2 = (f32[2,8,1326]{2,1,0:T(8,128)}, f32[2,8,1326]{2,1,0:T(8,128)S(1)}, u32[]{:S(2)}) copy-start(f32[2,8,1326]{2,1,0:T(8,128)S(1)} %fusion.20) | copy-start | bytes 254596
  103.1 4.5 %copy-start.15 = (pred[2]{0:T(512)(128)(4,1)S(1)}, pred[2]{0:T(512)(128)(4,1)}, u32[]{:S(2)}) copy-start(pred[2]{0:T(512)(128)(4,1)} %copy-done.14) | copy-start | bytes 10
  103.1 5.5 %copy-start.20 = (s32[4]{0:T(128)S(1)}, s32[4]{0:T(128)}, u32[]{:S(2)}) copy-start(s32[4]{0:T(128)} %param.17) | copy-start | bytes 52
  107.0 0.6 copy-start.3
  108.5 88.4 %all-reduce.2.cloned.1.call-start = ((), (), s32[]{:S(2)}) async-start(), calls=%async_computation.2 | async-start | bytes 180224 | tf_op jit(solution)/shard_map/psum | solution.py:90
Sparse Core Ops, SparseCore 0:
  108.7 34.8 all-gather.1
  155.9 41.0 all-reduce.1
